TPU v7x, 32 devices: a whole 2x2x4 slice. The times are simulated.
32 devices in a mesh: row: 2 (over y), col: 4 (over z), layer: 4 (over x, core).
Axes of the slice: x: 2, y: 2, z: 4, core: 2. Of those that a mesh axis runs over, the one named last changes fastest.
Arguments:
- density_tiles: bfloat16 [192, 4, 2, 128, 128], P(('row', 'col')), may hold values from -1.5 to 1.5
- tile_columns: int32 [192, 4, 2], P(('row', 'col')), may hold values from -1 to 191, as said below
Outputs:
- square_tiles: bfloat16 [192, 4, 2, 128, 128], P(('row', 'col'), None, None, 'layer')
Inputs may be any that keep to these rules, and one draw needn't show every extreme that they name: `tile_columns`: entry [i, g, s] is a tile column in group g (columns g * 48 to (g + 1) * 48 - 1) or -1; within one block row and group the listed columns are distinct and empty slots come after the listed ones; block row i lists its own column i in the first slot of its group, whose 2 slots are all listed; other groups hold 0 to 2 listed tiles.
All inputs are finite; a program needn't handle non-finite values.
Results may differ from a plain program's by a relative error of at most 0.0048.
Values may be sent and summed in bfloat16 or wider, within the bound.
A program may use at most 128 MiB of HBM per device.

v0:
```python
import jax
import jax.numpy as jnp
from jax import lax
from jax.sharding import PartitionSpec as P


def spread(value, axis, source):
    kept = jnp.where(lax.axis_index(axis) == source, value, 0).astype(value.dtype)
    return lax.psum(kept, axis)


def multiply(left_tiles, left_columns, right_tiles, right_columns, target_columns, start_row):
    is_live = left_columns >= 0
    inner_rows = jnp.where(is_live, left_columns - start_row, 0).astype(jnp.int32)
    inner_columns = right_columns[inner_rows]
    matches = (
        (inner_columns[:, :, None, :] == target_columns[:, None, :, None])
        & is_live[:, :, None, None]
        & (target_columns >= 0)[:, None, :, None]
    )
    slot_index = jnp.argmax(matches.astype(jnp.int32), axis=-1)
    located = jnp.any(matches, axis=-1)
    selected = right_tiles[inner_rows[:, :, None], slot_index]
    selected = jnp.where(located[:, :, :, None, None], selected, jnp.zeros((), jnp.bfloat16))
    return jnp.einsum("iarc,iascd->isrd", left_tiles, selected, preferred_element_type=jnp.float32)


def on_device(density_tiles, tile_columns):
    row_count = lax.axis_size("row")
    column_count = lax.axis_size("col")
    layer_count = lax.axis_size("layer")
    grid_tiles, grid_columns = (
        lax.all_to_all(density_tiles, "col", split_axis=1, concat_axis=0, tiled=True),
        lax.all_to_all(tile_columns, "col", split_axis=1, concat_axis=0, tiled=True),
    )
    block_tiles = grid_tiles[:, 0]
    block_columns = grid_columns[:, 0]
    group_rows = block_tiles.shape[0]
    row_ratio = column_count // row_count
    panel_rows = group_rows // row_ratio
    per_layer = column_count // layer_count
    layer_index = lax.axis_index("layer")
    partial_value = jnp.zeros(block_tiles.shape, jnp.float32)
    for panel_step in range(per_layer):
        panel_index = layer_index * per_layer + panel_step
        left_tiles, left_columns = (
            spread(block_tiles, "col", panel_index),
            spread(block_columns, "col", panel_index),
        )
        offset = panel_index % row_ratio * panel_rows
        part_tiles = lax.dynamic_slice_in_dim(block_tiles, offset, panel_rows, 0)
        part_columns = lax.dynamic_slice_in_dim(block_columns, offset, panel_rows, 0)
        right_tiles, right_columns = (
            spread(part_tiles, "row", panel_index // row_ratio),
            spread(part_columns, "row", panel_index // row_ratio),
        )
        partial_value = partial_value + multiply(
            left_tiles,
            left_columns,
            right_tiles,
            right_columns,
            block_columns,
            panel_index * panel_rows,
        )
    rounded = partial_value.astype(jnp.bfloat16)
    summed = lax.psum_scatter(
        rounded.astype(jnp.float32).astype(jnp.bfloat16), "layer", scatter_dimension=2, tiled=True
    )
    returned = lax.all_to_all(summed[:, None], "col", split_axis=0, concat_axis=1, tiled=True)
    return returned


def solution(mesh):
    in_specs = (P(("row", "col"), None, None, None, None), P(("row", "col"), None, None))
    out_specs = P(("row", "col"), None, None, "layer", None)
    return jax.shard_map(
        on_device, mesh=mesh, in_specs=in_specs, out_specs=out_specs, check_vma=False
    )
```

profile of v0, /device:TPU:0, one launch (start us, length us, event | category | flops | bytes accessed | tf_op | source)
XLA Modules:
  0.0 603.0 jit_solution(9816034779347705298)
XLA Ops:
  6.5 8.1 %copy.33 = bf16[24,4,2,128,128]{4,3,2,0,1:T(8,128)(2,1)} copy(bf16[24,4,2,128,128]{4,3,2,1,0:T(8,128)(2,1)} %param.2) | data formatting | bytes 12582912 | tf_op args[0]
  14.6 6.3 %all-to-all-start.1 = ((bf16[24,4,2,128,128]{4,3,2,0,1:T(8,128)(2,1)}), bf16[24,4,2,128,128]{4,3,2,0,1:T(8,128)(2,1)}, u32[]{:S(2)}, u32[]{:S(2)}) async-start(bf16[24,4,2,128,128]{4,3,2,0,1:T(8,128)(2,1)} %copy.33), calls=%async_computation.1 | async-start | bytes 12582912 | tf_op jit(solution)/shard_map/all_to_all | solution.py:33
  21.0 0.0 all-reduce.3.cloned.1.call-start
  21.0 138.7 %all-to-all-done.1 = bf16[24,4,2,128,128]{4,3,2,0,1:T(8,128)(2,1)} async-done(((bf16[24,4,2,128,128]{4,3,2,0,1:T(8,128)(2,1)}), bf16[24,4,2,128,128]{4,3,2,0,1:T(8,128)(2,1)}, u32[]{:S(2)}, u32[]{:S(2)}) %all-to-all-start.1) | async-done | bytes 6291488 | tf_op jit(solution)/shard_map/all_to_all | solution.py:33
  159.7 3.7 dynamic-slice_select_fusion
  163.4 0.0 all-reduce.3.cloned.1.call-update
  163.4 0.0 all-reduce.5.cloned.1.call-start
  163.5 6.3 %broadcast_select_fusion = bf16[96,2,128,128]{3,2,1,0:T(8,128)(2,1)} fusion(pred[]{:T(512)S(6)} %eq.26, bf16[24,4,2,128,128]{4,3,2,0,1:T(8,128)(2,1)} %all-to-all-done.1), kind=kLoop, calls=%fused_computation.9 | loop fusion | flops 3145728 | bytes 12582913 | tf_op jit(solution)/shard_map/jit(_where)/select_n | solution.py:8
  169.8 0.0 all-reduce.5.cloned.1.call-update
  169.9 3.3 all-to-all-start
  173.1 0.0 reduce-scatter.2.cloned.1.call-start
  173.2 5.5 all-to-all-done
  178.7 0.1 copy.27
  178.8 0.1 copy.31
  178.9 16.6 %psum.29 = s32[96,2]{1,0:T(8,128)S(1)} all-reduce(s32[96,2]{1,0:T(8,128)S(1)} %broadcast_select_fusion.1), channel_id=1, replica_groups=mesh['row'=2,'col'=4,'layer'=4] {'col'}, use_global_device_ids=true, to_apply=%region_1.2 | all-reduce | flops 192 | bytes 1536 | tf_op jit(solution)/shard_map/psum | solution.py:9
  195.6 0.1 copy.30
  195.6 0.1 copy.29
  195.8 0.1 reshape.19
  195.9 8.8 %psum.28 = s32[48,2]{1,0:T(8,128)S(1)} all-reduce(s32[48,2]{1,0:T(8,128)S(1)} %dynamic-slice_select_fusion.1), channel_id=1, replica_groups=mesh['row'=2,'col'=4,'layer'=4] {'row'}, use_global_device_ids=true, to_apply=%region_0.1 | all-reduce | flops 96 | bytes 768 | tf_op jit(solution)/shard_map/psum | solution.py:9
  204.7 0.7 gather_fusion
  205.4 0.1 copy.28
  205.5 0.1 copy.34
  205.6 0.6 iota_reduce_fusion
  206.2 0.1 copy.35
  206.4 0.2 reshape.25
  206.5 0.2 copy.32
  206.7 42.4 %all-reduce.3.cloned.1.call-done = bf16[48,2,128,128]{3,2,1,0:T(8,128)(2,1)} async-done(((bf16[48,2,128,128]{3,2,1,0:T(8,128)(2,1)}), bf16[48,2,128,128]{3,2,1,0:T(8,128)(2,1)}) %all-reduce.3.cloned.1.call-update) | async-done | bytes 3145744 | tf_op jit(solution)/shard_map/psum | solution.py:9
  249.1 18.2 %gather_fusion.1 = bf16[384,128,128]{2,1,0:T(8,128)(2,1)} fusion(bf16[48,2,128,128]{3,2,1,0:T(8,128)(2,1)} %all-reduce.3.cloned.1.call-done, s32[384]{0:T(512)S(1)} %reshape.25), kind=kCustom, calls=%fused_computation.1 | custom fusion | bytes 25168896 | tf_op jit(solution)/shard_map/gather | solution.py:23
  267.3 16.6 %copy.36 = bf16[96,2,2,128,128]{3,4,1,2,0:T(8,128)(2,1)} copy(bf16[96,2,2,128,128]{4,3,2,1,0:T(8,128)(2,1)} %bitcast.41) | data formatting | bytes 25165824 | tf_op jit(solution)/shard_map/gather | solution.py:23
  284.0 190.4 %all-reduce.5.cloned.1.call-done = bf16[96,2,128,128]{3,2,1,0:T(8,128)(2,1)} async-done(((bf16[96,2,128,128]{3,2,1,0:T(8,128)(2,1)}), bf16[96,2,128,128]{3,2,1,0:T(8,128)(2,1)}) %all-reduce.5.cloned.1.call-update) | async-done | bytes 6291472 | tf_op jit(solution)/shard_map/psum | solution.py:9
  474.4 10.0 %fusion.3 = bf16[96,2,128,128]{2,3,1,0:T(8,128)(2,1)} fusion(bf16[96,2,128,128]{3,2,1,0:T(8,128)(2,1)} %all-reduce.5.cloned.1.call-done, bf16[96,2,2,128,128]{3,4,1,2,0:T(8,128)(2,1)} %copy.36, pred[96,2,2]{1,2,0:T(4,128)(4,1)S(1)} %copy.32), kind=kOutput, calls=%fused_computation.6 | convolution fusion | flops 1620049920 | bytes 25166208 | tf_op jit(solution)/shard_map/iarc,iascd->isrd/dot_general | solution.py:25
  484.4 9.1 %copy.37 = bf16[96,2,128,128]{3,0,1,2:T(8,128)(2,1)} copy(bf16[96,2,128,128]{2,3,1,0:T(8,128)(2,1)} %fusion.3) | data formatting | bytes 12582912 | tf_op jit(solution)/shard_map/convert_element_type | solution.py:65
  493.5 0.0 reduce-scatter.2.cloned.1.call-update
  493.5 57.9 %reduce-scatter.2.cloned.1.call-done = bf16[96,2,32,128]{3,0,1,2:T(8,128)(2,1)} async-done(((bf16[96,2,128,128]{3,0,1,2:T(8,128)(2,1)}), bf16[96,2,32,128]{3,0,1,2:T(8,128)(2,1)}) %reduce-scatter.2.cloned.1.call-update) | async-done | bytes 1572880 | tf_op jit(solution)/shard_map/reduce_scatter | solution.py:66
  551.4 2.4 copy.38
  553.8 41.2 %all_to_all.48 = bf16[96,1,2,32,128]{4,3,2,1,0:T(8,128)(2,1)S(1)} all-to-all(bf16[96,1,2,32,128]{4,3,2,1,0:T(8,128)(2,1)S(1)} %copy.38), channel_id=1, replica_groups=mesh['row'=2,'col'=4,'layer'=4] {'col'}, dimensions={0} | all-to-all | bytes 3145728 | tf_op jit(solution)/shard_map/all_to_all | solution.py:69
  595.0 1.4 copy.43
  (8 shorter events, 0.1 us)
Async XLA Ops:
  14.6 145.1 %all-to-all-start.1 = ((bf16[24,4,2,128,128]{4,3,2,0,1:T(8,128)(2,1)}), bf16[24,4,2,128,128]{4,3,2,0,1:T(8,128)(2,1)}, u32[]{:S(2)}, u32[]{:S(2)}) async-start(bf16[24,4,2,128,128]{4,3,2,0,1:T(8,128)(2,1)} %copy.33), calls=%async_computation.1 | async-start | bytes 12582912 | tf_op jit(solution)/shard_map/all_to_all | solution.py:33
  21.0 228.1 %all-reduce.3.cloned.1.call-start = ((), (), s32[]{:S(2)}) async-start(), calls=%async_computation.4 | async-start | bytes 6291456 | tf_op jit(solution)/shard_map/psum | solution.py:9
  163.4 310.9 %all-reduce.5.cloned.1.call-start = ((), (), s32[]{:S(2)}) async-start(), calls=%async_computation.5 | async-start | bytes 12582912 | tf_op jit(solution)/shard_map/psum | solution.py:9
  169.9 8.8 %all-to-all-start = ((s32[24,4,2]{0,2,1:T(2,128)}), s32[24,4,2]{0,2,1:T(2,128)S(1)}, u32[]{:S(2)}, u32[]{:S(2)}) async-start(s32[24,4,2]{0,2,1:T(2,128)} %param.3), calls=%async_computation | async-start | bytes 8192 | tf_op jit(solution)/shard_map/all_to_all | solution.py:34
  173.1 378.3 %reduce-scatter.2.cloned.1.call-start = ((), (), s32[]{:S(2)}) async-start(), calls=%async_computation.6 | async-start | bytes 7864320 | tf_op jit(solution)/shard_map/reduce_scatter | solution.py:66
Sparse Core Ops, SparseCore 0:
  163.6 85.4 all-reduce.2
  251.5 222.8 all-reduce.4
  493.6 57.7 reduce-scatter.1
where the time goes:
time: 604 us; the launch traced here: 603 us
  waiting for transfers between devices  435 us (72%)
  blocking collectives  66.6 us (11%)
  local copies, waits for them, and re-layouts  57.7 us (10%)
  between operations  13.2 us (2%)
  other arithmetic  10.8 us (2%)
  matrix products  10 us (2%)
  starting transfers between devices  9.69 us (2%)
    psum x2, waiting for transfers between devices, spread(): return lax.psum(kept, axis)  233 us
    all_to_all x1, waiting for transfers between devices, on_device(): lax.all_to_all(density_tiles, 'col', split_axis=1, concat_axis=0, tiled=T...  139 us
    reduce_scatter x1, waiting for transfers between devices, on_device(): lax.psum_scatter(rounded.astype(jnp.float32).astype(jnp.bfloat16), 'layer...  57.9 us
    all_to_all x1, blocking collectives, on_device(): lax.all_to_all(summed[:, None], 'col', split_axis=0, concat_axis=1, tiled...  41.2 us
    gather x2, local copies, waits for them, and re-layouts, multiply(): selected = right_tiles[inner_rows[:, :, None], slot_index]  34.9 us
    psum x2, blocking collectives, spread(): return lax.psum(kept, axis)  25.4 us
  transfers between devices with their start and end apart: 5, of which 5 were waited for; matrix products, arithmetic and copies ran while one was open for 7% of the time, Pallas kernels for 0%

commit v1 on v0

--- a/solution.py
+++ b/solution.py
@@ -6,7 +6,7 @@
 
 def spread(value, axis, source):
     kept = jnp.where(lax.axis_index(axis) == source, value, 0).astype(value.dtype)
-    return lax.psum(kept, axis)
+    return jnp.sum(lax.all_gather(kept, axis), axis=0)
 
 
 def multiply(left_tiles, left_columns, right_tiles, right_columns, target_columns, start_row):

time: 604 us -> 817 us (1.35)
  waiting for transfers between devices: 435 us -> 655 us
  other arithmetic: 10.8 us -> 33.2 us
  local copies, waits for them, and re-layouts: 57.7 us -> 40.5 us
  blocking collectives: 66.6 us -> 53.7 us
    all_gather x0 -> x2, waiting for transfers between devices: none -> 454 us  [spread(): return jnp.sum(lax.all_gather(kept, axis), axis=0)]
    psum x2 -> x0, waiting for transfers between devices: 233 us -> none  [spread(): return lax.psum(kept, axis)]
    psum x2 -> x0, blocking collectives: 25.4 us -> none  [spread(): return lax.psum(kept, axis)]
    reduce_sum x0 -> x4, other arithmetic: none -> 22.6 us  [spread(): return jnp.sum(lax.all_gather(kept, axis), axis=0)]
    gather x2 -> x1, local copies, waits for them, and re-layouts: 34.9 us -> 17.7 us  [multiply(): selected = right_tiles[inner_rows[:, :, None], slot_index]]
    all_gather x0 -> x2, blocking collectives: none -> 12.5 us  [spread(): return jnp.sum(lax.all_gather(kept, axis), axis=0)]
  transfers between devices with their start and end apart: 5 -> 5, of which waited for: 5 -> 5; matrix products, arithmetic and copies ran while one was open for 7% -> 4% of each run, Pallas kernels for 0% -> 0%
where the time goes in v1:
time: 817 us; the launch traced here: 816 us
  waiting for transfers between devices  655 us (80%)
  blocking collectives  53.7 us (7%)
  local copies, waits for them, and re-layouts  40.5 us (5%)
  other arithmetic  33.2 us (4%)
  between operations  13.2 us (2%)
  matrix products  10.5 us (1%)
  starting transfers between devices  9.7 us (1%)
    all_gather x2, waiting for transfers between devices, spread(): return jnp.sum(lax.all_gather(kept, axis), axis=0)  454 us
    all_to_all x1, waiting for transfers between devices, on_device(): lax.all_to_all(density_tiles, 'col', split_axis=1, concat_axis=0, tiled=T...  139 us
    reduce_scatter x1, waiting for transfers between devices, on_device(): lax.psum_scatter(rounded.astype(jnp.float32).astype(jnp.bfloat16), 'layer...  57.2 us
    all_to_all x1, blocking collectives, on_device(): lax.all_to_all(summed[:, None], 'col', split_axis=0, concat_axis=1, tiled...  41.2 us
    reduce_sum x4, other arithmetic, spread(): return jnp.sum(lax.all_gather(kept, axis), axis=0)  22.6 us
    gather x1, local copies, waits for them, and re-layouts, multiply(): selected = right_tiles[inner_rows[:, :, None], slot_index]  17.7 us
  transfers between devices with their start and end apart: 5, of which 5 were waited for; matrix products, arithmetic and copies ran while one was open for 4% of the time, Pallas kernels for 0%

profile of v1, /device:TPU:0, one launch (start us, length us, event | category | flops | bytes accessed | tf_op | source)
XLA Modules:
  0.0 815.9 jit_solution(1746442794231038737)
XLA Ops:
  6.5 8.1 copy.43
  14.6 6.3 all-to-all-start.1
  21.0 0.0 all-gather.8.cloned.1.call-start
  21.0 138.7 %all-to-all-done.1 = bf16[24,4,2,128,128]{4,3,2,0,1:T(8,128)(2,1)} async-done(((bf16[24,4,2,128,128]{4,3,2,0,1:T(8,128)(2,1)}), bf16[24,4,2,128,128]{4,3,2,0,1:T(8,128)(2,1)}, u32[]{:S(2)}, u32[]{:S(2)}) %all-to-all-start.1) | async-done | bytes 6291488 | tf_op jit(solution)/shard_map/all_to_all | solution.py:33
  159.7 3.7 dynamic-slice_select_fusion
  163.4 0.0 all-gather.8.cloned.1.call-update
  163.5 0.0 all-gather.6.cloned.1.call-start
  163.5 5.9 bitcast_select_fusion
  169.4 0.0 all-gather.6.cloned.1.call-update
  169.4 3.3 all-to-all-start
  172.7 0.0 reduce-scatter.2.cloned.1.call-start
  172.8 5.5 all-to-all-done
  178.3 0.1 squeeze.6
  178.3 0.1 select_bitcast_fusion
  178.4 4.4 all-gather.2
  182.8 0.1 select_n.118
  182.9 8.1 all_gather.22
  191.1 0.1 copy.40
  191.2 0.1 copy.39
  191.3 0.1 reshape.77
  191.4 0.7 gather_fusion
  192.1 0.1 copy.41
  192.3 0.2 copy.42
  192.4 0.8 iota_reduce_fusion
  193.3 0.1 copy.44
  193.4 0.2 reshape.83
  193.6 49.6 %all-gather.8.cloned.1.call-done = bf16[96,2,128,128]{3,2,1,0:T(8,128)(2,1)} async-done(((bf16[48,2,128,128]{3,2,1,0:T(8,128)(2,1)}), bf16[96,2,128,128]{3,2,1,0:T(8,128)(2,1)}) %all-gather.8.cloned.1.call-update) | async-done | bytes 6291472 | tf_op jit(solution)/shard_map/all_gather | solution.py:9
  243.2 5.0 reduce_sum.44
  248.2 17.7 %gather_fusion.1 = bf16[384,128,128]{2,1,0:T(8,128)(2,1)} fusion(bf16[48,2,128,128]{3,2,1,0:T(8,128)(2,1)S(1)} %reduce_sum.44, s32[384]{0:T(512)S(1)} %reshape.83), kind=kCustom, calls=%fused_computation.1 | custom fusion | bytes 25168896 | tf_op jit(solution)/shard_map/gather | solution.py:23
  265.9 404.1 %all-gather.6.cloned.1.call-done = bf16[4,96,2,128,128]{4,3,2,1,0:T(8,128)(2,1)} async-done(((bf16[1,96,2,128,128]{4,3,2,1,0:T(8,128)(2,1)}), bf16[4,96,2,128,128]{4,3,2,1,0:T(8,128)(2,1)}) %all-gather.6.cloned.1.call-update) | async-done | bytes 25165840 | tf_op jit(solution)/shard_map/all_gather | solution.py:9
  669.9 17.5 %reduce_sum.45 = bf16[96,2,128,128]{3,2,1,0:T(8,128)(2,1)} reduce(bf16[4,96,2,128,128]{4,3,2,1,0:T(8,128)(2,1)} %all-gather.6.cloned.1.call-done, bf16[]{:T(256)} %constant.61.clone.1), dimensions={0}, to_apply=%region_5.6 | reduce | flops 9437184 | bytes 31457282 | tf_op jit(solution)/shard_map/reduce_sum | solution.py:9
  687.5 10.5 %fusion.3 = bf16[96,2,128,128]{2,3,1,0:T(8,128)(2,1)} fusion(bf16[96,2,128,128]{3,2,1,0:T(8,128)(2,1)} %reduce_sum.45, bf16[96,2,2,128,128]{4,3,2,1,0:T(8,128)(2,1)} %bitcast.56, pred[96,2,2]{2,1,0:T(4,128)(4,1)S(1)} %copy.42), kind=kOutput, calls=%fused_computation.6 | convolution fusion | flops 1620049920 | bytes 25166208 | tf_op jit(solution)/shard_map/iarc,iascd->isrd/dot_general | solution.py:25
  698.0 9.1 %copy.46 = bf16[96,2,128,128]{3,0,1,2:T(8,128)(2,1)} copy(bf16[96,2,128,128]{2,3,1,0:T(8,128)(2,1)} %fusion.3) | data formatting | bytes 12582912 | tf_op jit(solution)/shard_map/convert_element_type | solution.py:65
  707.1 0.0 reduce-scatter.2.cloned.1.call-update
  707.1 57.2 %reduce-scatter.2.cloned.1.call-done = bf16[96,2,32,128]{3,0,1,2:T(8,128)(2,1)} async-done(((bf16[96,2,128,128]{3,0,1,2:T(8,128)(2,1)}), bf16[96,2,32,128]{3,0,1,2:T(8,128)(2,1)}) %reduce-scatter.2.cloned.1.call-update) | async-done | bytes 1572880 | tf_op jit(solution)/shard_map/reduce_scatter | solution.py:66
  764.3 2.4 copy.47
  766.7 41.2 %all_to_all.48 = bf16[96,1,2,32,128]{4,3,2,1,0:T(8,128)(2,1)S(1)} all-to-all(bf16[96,1,2,32,128]{4,3,2,1,0:T(8,128)(2,1)S(1)} %copy.47), channel_id=1, replica_groups=mesh['row'=2,'col'=4,'layer'=4] {'col'}, dimensions={0} | all-to-all | bytes 3145728 | tf_op jit(solution)/shard_map/all_to_all | solution.py:69
  807.9 1.4 copy.54
  (12 shorter events, 0.1 us)
Async XLA Ops:
  14.6 145.1 %all-to-all-start.1 = ((bf16[24,4,2,128,128]{4,3,2,0,1:T(8,128)(2,1)}), bf16[24,4,2,128,128]{4,3,2,0,1:T(8,128)(2,1)}, u32[]{:S(2)}, u32[]{:S(2)}) async-start(bf16[24,4,2,128,128]{4,3,2,0,1:T(8,128)(2,1)} %copy.43), calls=%async_computation.1 | async-start | bytes 12582912 | tf_op jit(solution)/shard_map/all_to_all | solution.py:33
  21.0 222.2 %all-gather.8.cloned.1.call-start = ((), (), s32[]{:S(2)}) async-start(), calls=%async_computation.6 | async-start | bytes 9437184 | tf_op jit(solution)/shard_map/all_gather | solution.py:9
  163.5 506.5 %all-gather.6.cloned.1.call-start = ((), (), s32[]{:S(2)}) async-start(), calls=%async_computation.4 | async-start | bytes 31457280 | tf_op jit(solution)/shard_map/all_gather | solution.py:9
  169.4 8.8 %all-to-all-start = ((s32[24,4,2]{0,2,1:T(2,128)}), s32[24,4,2]{0,2,1:T(2,128)S(1)}, u32[]{:S(2)}, u32[]{:S(2)}) async-start(s32[24,4,2]{0,2,1:T(2,128)} %param.3), calls=%async_computation | async-start | bytes 8192 | tf_op jit(solution)/shard_map/all_to_all | solution.py:34
  172.7 591.6 %reduce-scatter.2.cloned.1.call-start = ((), (), s32[]{:S(2)}) async-start(), calls=%async_computation.5 | async-start | bytes 7864320 | tf_op jit(solution)/shard_map/reduce_scatter | solution.py:66
Sparse Core Ops, SparseCore 0:
  163.6 79.5 all-gather.7
  244.7 425.1 all-gather.5
  707.2 57.0 reduce-scatter.1
